TPU v7x, 32 devices: a whole 2x2x4 slice. The times are simulated.
32 devices in a mesh: gx: 4 (over y, x), gy: 8 (over z, core).
Axes of the slice: x: 2, y: 2, z: 4, core: 2. Of those that a mesh axis runs over, the one named last changes fastest.
Arguments:
- tokens: bfloat16 [4096, 8192], P('gy', 'gx'), may hold values from -6 to 6
- pair_ids: int32 [8], replicated, may hold values from 0 to 7, each once
- query_weight: bfloat16 [8192, 8192], P('gy', 'gx'), may hold values from -0.0625 to 0.0625
- key_matrix: bfloat16 [8192, 1024], P('gy', 'gx'), may hold values from -0.0625 to 0.0625
- value_matrix: bfloat16 [8192, 1024], P('gy', 'gx'), may hold values from -0.0625 to 0.0625
- query_bias: bfloat16 [8192], P('gx'), may hold values from -13 to 13
- key_bias: bfloat16 [1024], P('gx'), may hold values from -8 to 8
- value_offset_bias: bfloat16 [1024], P('gx'), may hold values from -3 to 3
Outputs:
- attn_out: bfloat16 [4096, 8192], P('gy', 'gx')
Inputs may be any that keep to these rules, and one draw needn't show every extreme that they name: `pair_ids`: each number from 0 to 7 appears once.
All inputs are finite; a program needn't handle non-finite values.
Results may differ from a plain program's by a relative error of at most 0.0055.
The roundings to bfloat16 on the way count: a program that leaves them out, or rounds other values in their place, can miss the bound.
Values may be sent and summed in bfloat16 or wider, within the bound.
A program may use at most 128 MiB of HBM per device.

v0:
```python
import math
import jax
import jax.numpy as jnp
from jax import lax
from jax.sharding import PartitionSpec as P

HEAD_SIZE = 128
rope_theta = 1000000.0
neg_large = -1e30


def table_lookup(entries, wanted):
    slot_ids = lax.iota(jnp.int32, entries.shape[0])
    return jnp.sum(jnp.where(wanted[:, None] == slot_ids[None, :], entries[None, :], 0), axis=1)


def layout_positions(pair_ids, total_row_count, tok_dev):
    half_len = tok_dev // 2
    row_ids = lax.iota(jnp.int32, total_row_count)
    within = row_ids % tok_dev
    owners = table_lookup(pair_ids, row_ids // tok_dev)
    mirrored = 2 * pair_ids.shape[0] - 1 - owners
    return jnp.where(
        within < half_len, owners * half_len + within, mirrored * half_len + within - half_len
    )


def apply_rotary(values, token_positions):
    half_size = values.shape[-1] // 2
    frequency = jnp.exp(
        lax.iota(jnp.float32, half_size) * (-2.0 * math.log(rope_theta) / values.shape[-1])
    )
    angles = token_positions.astype(jnp.float32)[:, None] * frequency[None, :]
    cos_part = jnp.cos(angles)[:, None, :]
    sin_part = jnp.sin(angles)[:, None, :]
    lower_half = values[..., :half_size]
    upper_half = values[..., half_size:]
    return jnp.concatenate(
        [
            lower_half * cos_part - upper_half * sin_part,
            upper_half * cos_part + lower_half * sin_part,
        ],
        axis=-1,
    )


def absorb(running, query_block, key_block, value_block, visible):
    row_peak, totals, outputs = running
    scale = 1.0 / math.sqrt(query_block.shape[-1])
    scores = (
        jnp.einsum("hqd,khd->hqk", query_block, key_block, preferred_element_type=jnp.float32)
        * scale
    )
    if visible is not None:
        scores = jnp.where(visible[None], scores, neg_large)
    new_peak = jnp.maximum(row_peak, jnp.max(scores, axis=-1))
    weights = jnp.exp(scores - new_peak[..., None])
    if visible is not None:
        weights = jnp.where(visible[None], weights, 0.0)
    rescale = jnp.exp(row_peak - new_peak)
    totals = totals * rescale + jnp.sum(weights, axis=-1)
    outputs = outputs * rescale[..., None] + jnp.einsum(
        "hqk,khd->hqd",
        weights.astype(jnp.bfloat16),
        value_block,
        preferred_element_type=jnp.float32,
    )
    return (new_peak, totals, outputs)


def on_device(
    tokens,
    pair_ids,
    query_weight,
    key_matrix,
    value_matrix,
    query_bias,
    key_bias,
    value_offset_bias,
):
    tok_dev = tokens.shape[0]
    half_len = tok_dev // 2
    whole_rows = tok_dev * lax.axis_size("gy")
    kv_local = key_matrix.shape[1] // HEAD_SIZE
    q_local = query_weight.shape[1] // HEAD_SIZE
    query_group_width = q_local // kv_local
    gathered = lax.all_gather(tokens, "gx", axis=1, tiled=True)
    stacked = jnp.concatenate([query_weight, key_matrix, value_matrix], axis=1)
    projected = jnp.dot(
        gathered,
        lax.all_gather(stacked, "gy", axis=0, tiled=True),
        preferred_element_type=jnp.float32,
    )
    all_positions = layout_positions(pair_ids, whole_rows, tok_dev)
    own_index = lax.axis_index("gy")
    own_positions = lax.dynamic_slice_in_dim(all_positions, own_index * tok_dev, tok_dev, 0)
    own_pair = table_lookup(pair_ids, jnp.reshape(own_index, (1,)))[0]
    q_cols = q_local * HEAD_SIZE
    kv_cols = kv_local * HEAD_SIZE
    queries = projected[:, :q_cols] + query_bias.astype(jnp.float32)
    queries = apply_rotary(queries.reshape(tok_dev, q_local, HEAD_SIZE), own_positions).astype(
        jnp.bfloat16
    )
    projected_key_rows = projected[:, q_cols : q_cols + kv_cols] + key_bias.astype(jnp.float32)
    projected_key_rows = (
        apply_rotary(projected_key_rows.reshape(tok_dev, kv_local, HEAD_SIZE), own_positions)
        .astype(jnp.bfloat16)
        .reshape(tok_dev, kv_cols)
    )
    projected_value_rows = (
        projected[:, q_cols + kv_cols :] + value_offset_bias.astype(jnp.float32)
    ).astype(jnp.bfloat16)
    query_rows = (
        queries.reshape(tok_dev, kv_local, query_group_width, HEAD_SIZE)
        .transpose(1, 0, 2, 3)
        .reshape(kv_local, tok_dev * query_group_width, HEAD_SIZE)
    )
    row_positions = jnp.repeat(own_positions, query_group_width)
    row_total = tok_dev * query_group_width
    initial = (
        jnp.full((kv_local, row_total), neg_large, jnp.float32),
        jnp.zeros((kv_local, row_total), jnp.float32),
        jnp.zeros((kv_local, row_total, HEAD_SIZE), jnp.float32),
    )

    def paired(running, key_shard, value_shard, earlier):
        cut_rows = half_len * query_group_width
        former = tuple((member[:, :cut_rows] for member in running))
        latter = tuple((member[:, cut_rows:] for member in running))
        query_former = query_rows[:, :cut_rows]
        query_latter = query_rows[:, cut_rows:]
        latter = absorb(latter, query_latter, key_shard[:half_len], value_shard[:half_len], None)
        picked_state = tuple(
            (jnp.where(earlier, left, right) for left, right in zip(former, latter))
        )
        query_pick = jnp.where(earlier, query_former, query_latter)
        key_pick = jnp.where(earlier, key_shard[:half_len], key_shard[half_len:])
        value_pick = jnp.where(earlier, value_shard[:half_len], value_shard[half_len:])
        updated = absorb(picked_state, query_pick, key_pick, value_pick, None)
        former = tuple((jnp.where(earlier, fresh, kept) for fresh, kept in zip(updated, former)))
        latter = tuple((jnp.where(earlier, kept, fresh) for fresh, kept in zip(updated, latter)))
        return tuple(
            (jnp.concatenate([left, right], axis=1) for left, right in zip(former, latter))
        )

    key_piece = lax.all_gather(projected_key_rows, "gy", axis=0, tiled=True)
    value_piece = lax.all_gather(projected_value_rows, "gy", axis=0, tiled=True)
    total_row_count = key_piece.shape[0]

    def one_shard(shard_index, carried):
        begin = shard_index * tok_dev
        key_shard = lax.dynamic_slice_in_dim(key_piece, begin, tok_dev, 0).reshape(
            tok_dev, kv_local, HEAD_SIZE
        )
        value_shard = lax.dynamic_slice_in_dim(value_piece, begin, tok_dev, 0).reshape(
            tok_dev, kv_local, HEAD_SIZE
        )
        source = jnp.reshape(begin // tok_dev, (1,))
        their_pair = table_lookup(pair_ids, source)[0]

        def itself(state_in):
            key_positions = lax.dynamic_slice_in_dim(all_positions, begin, tok_dev, 0)
            visible = key_positions[None, :] <= row_positions[:, None]
            return absorb(state_in, query_rows, key_shard, value_shard, visible)

        def elsewhere(state_in):
            return paired(state_in, key_shard, value_shard, their_pair < own_pair)

        return lax.cond(their_pair == own_pair, itself, elsewhere, carried)

    row_peak, totals, outputs = lax.fori_loop(0, total_row_count // tok_dev, one_shard, initial)
    normalized = (outputs / totals[..., None]).astype(jnp.bfloat16)
    return (
        normalized.reshape(kv_local, tok_dev, query_group_width, HEAD_SIZE)
        .transpose(1, 0, 2, 3)
        .reshape(tok_dev, q_cols)
    )


def solution(mesh):
    in_specs = (
        P("gy", "gx"),
        P(),
        P("gy", "gx"),
        P("gy", "gx"),
        P("gy", "gx"),
        P("gx"),
        P("gx"),
        P("gx"),
    )
    out_specs = P("gy", "gx")
    return jax.shard_map(
        on_device, mesh=mesh, in_specs=in_specs, out_specs=out_specs, check_vma=False
    )
```

profile of v0, /device:TPU:0, one launch (start us, length us, event | category | flops | bytes accessed | tf_op | source)
XLA Modules:
  0.0 768.3 jit_solution(7641844237663635094)
XLA Ops:
  7.3 6.9 pad_maximum_fusion.3
  15.7 83.8 %all-gather.7.cloned.1.call-done = bf16[512,8192]{1,0:T(8,128)(2,1)} async-done(((bf16[512,2048]{1,0:T(8,128)(2,1)}), bf16[512,8192]{1,0:T(8,128)(2,1)}) %all-gather.7.cloned.1.call-update) | async-done | bytes 8388624 | tf_op jit(solution)/shard_map/all_gather | solution.py:87
  99.4 360.5 %all-gather.5.cloned.1.call-done = bf16[8192,2560]{1,0:T(8,128)(2,1)} async-done(((bf16[1024,2560]{1,0:T(8,128)(2,1)}), bf16[8192,2560]{1,0:T(8,128)(2,1)}) %all-gather.5.cloned.1.call-update) | async-done | bytes 41943056 | tf_op jit(solution)/shard_map/all_gather | solution.py:91
  459.9 30.0 %convolution_bitcast_fusion = f32[512,2560]{0,1:T(8,128)} fusion(bf16[8192,2560]{1,0:T(8,128)(2,1)} %all-gather.5.cloned.1.call-done, bf16[512,8192]{1,0:T(8,128)(2,1)} %all-gather.7.cloned.1.call-done), kind=kOutput, calls=%fused_computation.67 | convolution fusion | flops 21474836480 | bytes 55574528 | tf_op jit(solution)/shard_map/dot_general | solution.py:89
  489.9 2.0 fusion.42
  494.0 2.5 slice_add_fusion
  496.5 1.7 subtract_convert_fusion
  498.2 2.7 copy.34
  500.9 2.5 copy.35
  503.4 4.1 maximum_bitcast_fusion
  507.5 13.1 %all-gather.9.cloned.1.call-done = bf16[4096,256]{0,1:T(8,128)(2,1)} async-done(((bf16[512,256]{0,1:T(8,128)(2,1)}), bf16[4096,256]{0,1:T(8,128)(2,1)}) %all-gather.9.cloned.1.call-update) | async-done | bytes 2097168 | tf_op jit(solution)/shard_map/all_gather | solution.py:146
  520.6 30.0 %all-gather.11.cloned.1.call-done = bf16[4096,256]{0,1:T(8,128)(2,1)} async-done(((bf16[512,256]{0,1:T(8,128)(2,1)}), bf16[4096,256]{0,1:T(8,128)(2,1)}) %all-gather.11.cloned.1.call-update) | async-done | bytes 2097168 | tf_op jit(solution)/shard_map/all_gather | solution.py:147
  550.7 2.2 broadcast_in_dim.85
  553.5 203.1 %while.20 = (s32[]{:T(128)}, f32[2,4096]{1,0:T(2,128)S(1)}, f32[2,4096]{1,0:T(2,128)}, f32[2,4096,128]{2,1,0:T(8,128)}, s32[8]{0:T(128)S(1)}, /*index=5*/s32[]{:...) while((s32[]{:T(128)}, f32[2,4096]{1,0:T(2,128)S(1)}, ...), condition=%wide.region_12.13_spmd.clone, body=%wide.region_2.12_spmd.clone.sunk | while | flops 2206220288 | bytes 138748624 | solution.py:171
  556.6 28.6 %conditional.3 = (f32[2,4096]{1,0:T(2,128)}, f32[2,4096]{1,0:T(2,128)}, f32[2,4096,128]{2,1,0:T(8,128)}) conditional(s32[]{:T(128)} %convert_element_type.69, (s32[]{:T(128)}, s32[]{:T(128)}, f32[2,4096]{1,0:T(2,128)S(1)}, bf16[2,4096,128]{2,1,0:T(8,128)(2,1)}, bf16[512,2,128]{0,2,1:T(8,128)(2,1)S(1)}, /*index=5*/f32[2,4096]{1,0:T(2,128)}, ...), branch_computations={%region_4.8_spmd, %region_9.11_spmd} | conditional | flops 2206220288 | bytes 137633952 | solution.py:169
  558.3 5.8 fusion.28
  564.2 1.9 max.8
  566.1 5.3 fusion.30
  572.9 12.3 %fusion.34 = f32[2,4096,128]{2,1,0:T(8,128)} fusion(bf16[512,2,128]{0,2,1:T(8,128)(2,1)S(1)} %get-tuple-element.414, f32[2,4096,512]{1,2,0:T(8,128)} %copy-done.3, f32[2,4096]{1,0:T(2,128)} %max.8, pred[4096,512]{0,1:T(8,128)(4,1)S(1)} %broadcast_compare_fusion, f32[2,4096,128]{2,1,0:T(8,128)} %get-tuple-element.321, f32[2,4096]{1,0:T(2,128)S(1)} %get-tuple-element.446), kind=kOutput, calls=%fused_computation.55 | convolution fusion | flops 1096810496 | bytes 27590656 | tf_op jit(solution)/shard_map/while/body/eval_jaxpr/cond/branch_1_fun/hqk,khd->hqd/dot_general | solution.py:62
  589.0 20.6 %conditional.3 = (f32[2,4096]{1,0:T(2,128)}, f32[2,4096]{1,0:T(2,128)}, f32[2,4096,128]{2,1,0:T(8,128)}) conditional(s32[]{:T(128)} %convert_element_type.69, (s32[]{:T(128)}, s32[]{:T(128)}, f32[2,4096]{1,0:T(2,128)S(1)}, bf16[2,4096,128]{2,1,0:T(8,128)(2,1)}, bf16[512,2,128]{0,2,1:T(8,128)(2,1)S(1)}, /*index=5*/f32[2,4096]{1,0:T(2,128)}, ...), branch_computations={%region_4.8_spmd, %region_9.11_spmd} | conditional | flops 2206220288 | bytes 137633952 | solution.py:169
  590.4 2.3 multiply_reduce_fusion
  592.7 2.8 multiply_reduce_fusion.1
  598.4 4.4 convolution_add_fusion.1
  603.7 1.6 slice_select_fusion
  605.4 2.2 pad_maximum_fusion
  613.4 20.6 %conditional.3 = (f32[2,4096]{1,0:T(2,128)}, f32[2,4096]{1,0:T(2,128)}, f32[2,4096,128]{2,1,0:T(8,128)}) conditional(s32[]{:T(128)} %convert_element_type.69, (s32[]{:T(128)}, s32[]{:T(128)}, f32[2,4096]{1,0:T(2,128)S(1)}, bf16[2,4096,128]{2,1,0:T(8,128)(2,1)}, bf16[512,2,128]{0,2,1:T(8,128)(2,1)S(1)}, /*index=5*/f32[2,4096]{1,0:T(2,128)}, ...), branch_computations={%region_4.8_spmd, %region_9.11_spmd} | conditional | flops 2206220288 | bytes 137633952 | solution.py:169
  614.8 2.3 multiply_reduce_fusion
  617.1 2.8 multiply_reduce_fusion.1
  619.9 1.5 fusion.3
  622.8 4.4 convolution_add_fusion.1
  628.1 1.6 slice_select_fusion
  629.8 2.2 pad_maximum_fusion
  637.8 20.6 %conditional.3 = (f32[2,4096]{1,0:T(2,128)}, f32[2,4096]{1,0:T(2,128)}, f32[2,4096,128]{2,1,0:T(8,128)}) conditional(s32[]{:T(128)} %convert_element_type.69, (s32[]{:T(128)}, s32[]{:T(128)}, f32[2,4096]{1,0:T(2,128)S(1)}, bf16[2,4096,128]{2,1,0:T(8,128)(2,1)}, bf16[512,2,128]{0,2,1:T(8,128)(2,1)S(1)}, /*index=5*/f32[2,4096]{1,0:T(2,128)}, ...), branch_computations={%region_4.8_spmd, %region_9.11_spmd} | conditional | flops 2206220288 | bytes 137633952 | solution.py:169
  639.2 2.3 multiply_reduce_fusion
  641.5 2.8 multiply_reduce_fusion.1
  647.2 4.4 convolution_add_fusion.1
  652.5 1.6 slice_select_fusion
  654.2 2.2 pad_maximum_fusion
  662.2 20.6 %conditional.3 = (f32[2,4096]{1,0:T(2,128)}, f32[2,4096]{1,0:T(2,128)}, f32[2,4096,128]{2,1,0:T(8,128)}) conditional(s32[]{:T(128)} %convert_element_type.69, (s32[]{:T(128)}, s32[]{:T(128)}, f32[2,4096]{1,0:T(2,128)S(1)}, bf16[2,4096,128]{2,1,0:T(8,128)(2,1)}, bf16[512,2,128]{0,2,1:T(8,128)(2,1)S(1)}, /*index=5*/f32[2,4096]{1,0:T(2,128)}, ...), branch_computations={%region_4.8_spmd, %region_9.11_spmd} | conditional | flops 2206220288 | bytes 137633952 | solution.py:169
  663.6 2.3 multiply_reduce_fusion
  665.9 2.8 multiply_reduce_fusion.1
  671.6 4.4 convolution_add_fusion.1
  676.9 1.6 slice_select_fusion
  678.6 2.2 pad_maximum_fusion
  686.6 20.6 %conditional.3 = (f32[2,4096]{1,0:T(2,128)}, f32[2,4096]{1,0:T(2,128)}, f32[2,4096,128]{2,1,0:T(8,128)}) conditional(s32[]{:T(128)} %convert_element_type.69, (s32[]{:T(128)}, s32[]{:T(128)}, f32[2,4096]{1,0:T(2,128)S(1)}, bf16[2,4096,128]{2,1,0:T(8,128)(2,1)}, bf16[512,2,128]{0,2,1:T(8,128)(2,1)S(1)}, /*index=5*/f32[2,4096]{1,0:T(2,128)}, ...), branch_computations={%region_4.8_spmd, %region_9.11_spmd} | conditional | flops 2206220288 | bytes 137633952 | solution.py:169
  688.0 2.3 multiply_reduce_fusion
  690.3 2.8 multiply_reduce_fusion.1
  696.0 4.4 convolution_add_fusion.1
  701.3 1.6 slice_select_fusion
  702.9 2.2 pad_maximum_fusion
  710.9 20.6 %conditional.3 = (f32[2,4096]{1,0:T(2,128)}, f32[2,4096]{1,0:T(2,128)}, f32[2,4096,128]{2,1,0:T(8,128)}) conditional(s32[]{:T(128)} %convert_element_type.69, (s32[]{:T(128)}, s32[]{:T(128)}, f32[2,4096]{1,0:T(2,128)S(1)}, bf16[2,4096,128]{2,1,0:T(8,128)(2,1)}, bf16[512,2,128]{0,2,1:T(8,128)(2,1)S(1)}, /*index=5*/f32[2,4096]{1,0:T(2,128)}, ...), branch_computations={%region_4.8_spmd, %region_9.11_spmd} | conditional | flops 2206220288 | bytes 137633952 | solution.py:169
  712.4 2.3 multiply_reduce_fusion
  714.7 2.8 multiply_reduce_fusion.1
  720.4 4.4 convolution_add_fusion.1
  725.7 1.6 slice_select_fusion
  727.3 2.2 pad_maximum_fusion
  735.3 20.6 %conditional.3 = (f32[2,4096]{1,0:T(2,128)}, f32[2,4096]{1,0:T(2,128)}, f32[2,4096,128]{2,1,0:T(8,128)}) conditional(s32[]{:T(128)} %convert_element_type.69, (s32[]{:T(128)}, s32[]{:T(128)}, f32[2,4096]{1,0:T(2,128)S(1)}, bf16[2,4096,128]{2,1,0:T(8,128)(2,1)}, bf16[512,2,128]{0,2,1:T(8,128)(2,1)S(1)}, /*index=5*/f32[2,4096]{1,0:T(2,128)}, ...), branch_computations={%region_4.8_spmd, %region_9.11_spmd} | conditional | flops 2206220288 | bytes 137633952 | solution.py:169
  736.8 2.3 multiply_reduce_fusion
  739.1 2.8 multiply_reduce_fusion.1
  744.8 4.4 convolution_add_fusion.1
  750.1 1.6 slice_select_fusion
  751.7 2.2 pad_maximum_fusion
  756.7 2.9 fusion.41
  760.0 1.9 copy.44
  (177 shorter events, 68.9 us)
Async XLA Ops:
  6.5 92.9 %all-gather.7.cloned.1.call-start = ((), (), s32[]{:S(2)}) async-start(), calls=%async_computation.1 | async-start | bytes 10485760 | tf_op jit(solution)/shard_map/all_gather | solution.py:87
  7.3 452.7 %all-gather.5.cloned.1.call-start = ((), (), s32[]{:S(2)}) async-start(), calls=%async_computation | async-start | bytes 47185920 | tf_op jit(solution)/shard_map/all_gather | solution.py:91
  14.2 0.7 copy-start.9
  14.2 0.7 copy-start.10
  14.2 0.7 copy-start.8
  14.2 506.4 %all-gather.9.cloned.1.call-start = ((), (), s32[]{:S(2)}) async-start(), calls=%async_computation.2 | async-start | bytes 2359296 | tf_op jit(solution)/shard_map/all_gather | solution.py:146
  15.6 477.7 %copy-start.7 = (bf16[2048]{0:T(1024)(128)(2,1)S(1)}, bf16[2048]{0:T(1024)(128)(2,1)}, u32[]{:S(2)}) copy-start(bf16[2048]{0:T(1024)(128)(2,1)} %param.17) | copy-start | bytes 12292
  492.8 57.9 %all-gather.11.cloned.1.call-start = ((), (), s32[]{:S(2)}) async-start(), calls=%async_computation.3 | async-start | bytes 2359296 | tf_op jit(solution)/shard_map/all_gather | solution.py:147
  556.6 1.7 copy-start.5
  564.2 7.2 copy-start.3
  566.1 5.3 copy-start.6
  592.7 4.3 copy-start
  595.5 2.0 copy-start.2
  598.4 4.4 copy-start.1
  598.4 5.3 copy-start.4
  617.1 4.3 copy-start
  619.9 2.0 copy-start.2
  622.8 4.4 copy-start.1
  622.8 5.3 copy-start.4
  641.5 4.3 copy-start
  644.3 2.0 copy-start.2
  647.2 4.4 copy-start.1
  647.2 5.3 copy-start.4
  665.9 4.3 copy-start
  668.6 2.0 copy-start.2
  671.6 4.4 copy-start.1
  671.6 5.3 copy-start.4
  690.3 4.3 copy-start
  693.0 2.0 copy-start.2
  696.0 4.4 copy-start.1
  696.0 5.3 copy-start.4
  714.7 4.3 copy-start
  717.4 2.0 copy-start.2
  720.4 4.4 copy-start.1
  720.4 5.3 copy-start.4
  739.0 4.3 copy-start
  741.8 2.0 copy-start.2
  744.8 4.4 copy-start.1
  744.8 5.3 copy-start.4
Sparse Core Ops, SparseCore 0:
  9.2 90.1 all-gather.6
  101.1 358.8 all-gather.4
  492.9 27.7 all-gather.8
  522.1 28.5 all-gather.10
where the time goes:
time: 771 us; the launch traced here: 768 us
  waiting for transfers between devices  489 us (63%)
  matrix products  126 us (16%)
  other arithmetic  83.3 us (11%)
  local copies, waits for them, and re-layouts  37.8 us (5%)
  loops' own time  19.6 us (3%)
  between operations  13.2 us (2%)
    all_gather x1, waiting for transfers between devices, on_device(): lax.all_gather(stacked, 'gy', axis=0, tiled=True)  361 us
    all_gather x1, waiting for transfers between devices, on_device(): gathered = lax.all_gather(tokens, 'gx', axis=1, tiled=True)  83.8 us
    dot_general x15, matrix products, absorb(): jnp.einsum('hqk,khd->hqd', weights.astype(jnp.bfloat16), value_block, pre...  54.5 us
    dot_general x15, matrix products, absorb(): jnp.einsum('hqd,khd->hqk', query_block, key_block, preferred_element_type...  41.1 us
    all_gather x1, waiting for transfers between devices, on_device(): value_piece = lax.all_gather(projected_value_rows, 'gy', axis=0, tiled=True)  30 us
    dot_general x1, matrix products, on_device(): jnp.dot(gathered, lax.all_gather(stacked, 'gy', axis=0, tiled=True), pref...  30 us
    concatenate x21, other arithmetic, paired(): jnp.concatenate([left, right], axis=1)  24.3 us
    reduce_sum x8, other arithmetic, absorb(): totals = totals * rescale + jnp.sum(weights, axis=-1)  15.5 us
  transfers between devices with their start and end apart: 4, of which 4 were waited for; matrix products, arithmetic and copies ran while one was open for 3% of the time, Pallas kernels for 0%

commit v1 on v0

--- a/solution.py
+++ b/solution.py
@@ -7,6 +7,9 @@
 HEAD_SIZE = 128
 rope_theta = 1000000.0
 neg_large = -1e30
+start_ticks = lambda payload, in_dim: jnp.concatenate(
+    lax.all_to_all(jnp.stack([payload] * lax.axis_size("gy")), "gy", 0, 0), axis=in_dim
+)
 
 
 def table_lookup(entries, wanted):
@@ -86,11 +89,7 @@
     query_group_width = q_local // kv_local
     gathered = lax.all_gather(tokens, "gx", axis=1, tiled=True)
     stacked = jnp.concatenate([query_weight, key_matrix, value_matrix], axis=1)
-    projected = jnp.dot(
-        gathered,
-        lax.all_gather(stacked, "gy", axis=0, tiled=True),
-        preferred_element_type=jnp.float32,
-    )
+    projected = jnp.dot(gathered, start_ticks(stacked, 0), preferred_element_type=jnp.float32)
     all_positions = layout_positions(pair_ids, whole_rows, tok_dev)
     own_index = lax.axis_index("gy")
     own_positions = lax.dynamic_slice_in_dim(all_positions, own_index * tok_dev, tok_dev, 0)

time: 771 us -> 1250 us (1.62)
  waiting for transfers between devices: 489 us -> 947 us
  local copies, waits for them, and re-layouts: 37.8 us -> 51 us
    all_to_all x0 -> x1, waiting for transfers between devices: none -> 811 us  [lax.all_to_all(jnp.stack([payload] * lax.axis_size('gy')), 'gy', 0, 0)]
    all_gather x1 -> x0, waiting for transfers between devices: 361 us -> none  [on_device(): lax.all_gather(stacked, 'gy', axis=0, tiled=True)]
    another operation x14 -> x15, local copies, waits for them, and re-layouts: 2.36 us -> 16.2 us  [the longest x1 13.8 us: jnp.stack([payload] * lax.axis_size('gy'))]
  transfers between devices with their start and end apart: 4 -> 4, of which waited for: 4 -> 4; matrix products, arithmetic and copies ran while one was open for 3% -> 1% of each run, Pallas kernels for 0% -> 0%
where the time goes in v1:
time: 1250 us
  waiting for transfers between devices  947 us (76%)
  matrix products  126 us (10%)
  other arithmetic  80.3 us (6%)
  local copies, waits for them, and re-layouts  51 us (4%)
  loops' own time  19.6 us (2%)
  between operations  13.3 us (1%)
    all_to_all x1, waiting for transfers between devices, lax.all_to_all(jnp.stack([payload] * lax.axis_size('gy')), 'gy', 0, 0)  811 us
    all_gather x1, waiting for transfers between devices, on_device(): gathered = lax.all_gather(tokens, 'gx', axis=1, tiled=True)  91.4 us
    dot_general x15, matrix products, absorb(): jnp.einsum('hqk,khd->hqd', weights.astype(jnp.bfloat16), value_block, pre...  54.5 us
    dot_general x15, matrix products, absorb(): jnp.einsum('hqd,khd->hqk', query_block, key_block, preferred_element_type...  41.1 us
    all_gather x1, waiting for transfers between devices, on_device(): value_piece = lax.all_gather(projected_value_rows, 'gy', axis=0, tiled=True)  30.2 us
    dot_general x1, matrix products, on_device(): jnp.dot(gathered, start_ticks(stacked, 0), preferred_element_type=jnp.flo...  30 us
  transfers between devices with their start and end apart: 4, of which 4 were waited for; matrix products, arithmetic and copies ran while one was open for 1% of the time, Pallas kernels for 0%

profile of v1, /device:TPU:0, one launch (start us, length us, event | category | flops | bytes accessed | tf_op | source)
XLA Modules:
  0.0 1245.5 jit_solution(17334891910721846979)
XLA Ops:
  6.5 4.5 pad_maximum_fusion.3
  11.0 13.8 %stack.2 = bf16[8,1024,2560]{2,1,0:T(8,128)(2,1)} broadcast(bf16[1024,2560]{1,0:T(8,128)(2,1)S(1)} %pad_maximum_fusion.3), dimensions={1,2} | broadcast | bytes 47185920 | tf_op jit(solution)/shard_map/stack | solution.py:11
  24.8 7.9 all-to-all-start
  34.4 91.4 %all-gather.4.cloned.1.call-done = bf16[512,8192]{1,0:T(8,128)(2,1)} async-done(((bf16[512,2048]{1,0:T(8,128)(2,1)}), bf16[512,8192]{1,0:T(8,128)(2,1)}) %all-gather.4.cloned.1.call-update) | async-done | bytes 8388624 | tf_op jit(solution)/shard_map/all_gather | solution.py:90
  125.8 810.8 %all-to-all-done = bf16[8,1024,2560]{2,1,0:T(8,128)(2,1)} async-done(((bf16[8,1024,2560]{2,1,0:T(8,128)(2,1)}), bf16[8,1024,2560]{2,1,0:T(8,128)(2,1)}, u32[]{:S(2)}, u32[]{:S(2)}) %all-to-all-start) | async-done | bytes 41943072 | tf_op jit(solution)/shard_map/all_to_all | solution.py:11
  936.7 30.0 %convolution_bitcast_fusion = f32[512,2560]{0,1:T(8,128)} fusion(bf16[8192,2560]{1,0:T(8,128)(2,1)} %bitcast, bf16[512,8192]{1,0:T(8,128)(2,1)} %all-gather.4.cloned.1.call-done), kind=kOutput, calls=%fused_computation.67 | convolution fusion | flops 21474836480 | bytes 55574528 | tf_op jit(solution)/shard_map/dot_general | solution.py:92
  966.7 2.0 fusion.42
  971.0 2.5 slice_add_fusion
  973.5 1.7 subtract_convert_fusion
  975.2 2.7 copy.34
  977.9 2.5 copy.35
  980.4 4.1 maximum_bitcast_fusion
  984.5 13.8 %all-gather.6.cloned.1.call-done = bf16[4096,256]{0,1:T(8,128)(2,1)} async-done(((bf16[512,256]{0,1:T(8,128)(2,1)}), bf16[4096,256]{0,1:T(8,128)(2,1)}) %all-gather.6.cloned.1.call-update) | async-done | bytes 2097168 | tf_op jit(solution)/shard_map/all_gather | solution.py:145
  998.3 30.2 %all-gather.8.cloned.1.call-done = bf16[4096,256]{0,1:T(8,128)(2,1)} async-done(((bf16[512,256]{0,1:T(8,128)(2,1)}), bf16[4096,256]{0,1:T(8,128)(2,1)}) %all-gather.8.cloned.1.call-update) | async-done | bytes 2097168 | tf_op jit(solution)/shard_map/all_gather | solution.py:146
  1028.5 2.2 broadcast_in_dim.85
  1031.4 202.5 %while.20 = (s32[]{:T(128)}, f32[2,4096]{1,0:T(2,128)S(1)}, f32[2,4096]{1,0:T(2,128)}, f32[2,4096,128]{2,1,0:T(8,128)}, s32[8]{0:T(128)S(1)}, /*index=5*/s32[]{:...) while((s32[]{:T(128)}, f32[2,4096]{1,0:T(2,128)S(1)}, ...), condition=%wide.region_12.13_spmd.clone, body=%wide.region_2.12_spmd.clone.sunk | while | flops 2206220288 | bytes 138748624 | solution.py:170
  1034.3 28.6 %conditional.3 = (f32[2,4096]{1,0:T(2,128)}, f32[2,4096]{1,0:T(2,128)}, f32[2,4096,128]{2,1,0:T(8,128)}) conditional(s32[]{:T(128)} %convert_element_type.69, (s32[]{:T(128)}, s32[]{:T(128)}, f32[2,4096]{1,0:T(2,128)S(1)}, bf16[2,4096,128]{2,1,0:T(8,128)(2,1)}, bf16[512,2,128]{0,2,1:T(8,128)(2,1)S(1)}, /*index=5*/f32[2,4096]{1,0:T(2,128)}, ...), branch_computations={%region_4.8_spmd, %region_9.11_spmd} | conditional | flops 2206220288 | bytes 137633952 | solution.py:168
  1036.0 5.8 fusion.28
  1041.9 1.9 max.8
  1043.8 5.3 fusion.30
  1050.6 12.3 fusion.34
  1066.7 20.6 %conditional.3 = (f32[2,4096]{1,0:T(2,128)}, f32[2,4096]{1,0:T(2,128)}, f32[2,4096,128]{2,1,0:T(8,128)}) conditional(s32[]{:T(128)} %convert_element_type.69, (s32[]{:T(128)}, s32[]{:T(128)}, f32[2,4096]{1,0:T(2,128)S(1)}, bf16[2,4096,128]{2,1,0:T(8,128)(2,1)}, bf16[512,2,128]{0,2,1:T(8,128)(2,1)S(1)}, /*index=5*/f32[2,4096]{1,0:T(2,128)}, ...), branch_computations={%region_4.8_spmd, %region_9.11_spmd} | conditional | flops 2206220288 | bytes 137633952 | solution.py:168
  1068.1 2.3 multiply_reduce_fusion
  1070.4 2.8 multiply_reduce_fusion.1
  1076.1 4.4 convolution_add_fusion.1
  1081.4 1.6 slice_select_fusion
  1083.1 2.2 pad_maximum_fusion
  1091.0 20.6 %conditional.3 = (f32[2,4096]{1,0:T(2,128)}, f32[2,4096]{1,0:T(2,128)}, f32[2,4096,128]{2,1,0:T(8,128)}) conditional(s32[]{:T(128)} %convert_element_type.69, (s32[]{:T(128)}, s32[]{:T(128)}, f32[2,4096]{1,0:T(2,128)S(1)}, bf16[2,4096,128]{2,1,0:T(8,128)(2,1)}, bf16[512,2,128]{0,2,1:T(8,128)(2,1)S(1)}, /*index=5*/f32[2,4096]{1,0:T(2,128)}, ...), branch_computations={%region_4.8_spmd, %region_9.11_spmd} | conditional | flops 2206220288 | bytes 137633952 | solution.py:168
  1092.4 2.3 multiply_reduce_fusion
  1094.7 2.8 multiply_reduce_fusion.1
  1100.4 4.4 convolution_add_fusion.1
  1105.7 1.6 slice_select_fusion
  1107.4 2.2 pad_maximum_fusion
  1115.3 20.6 %conditional.3 = (f32[2,4096]{1,0:T(2,128)}, f32[2,4096]{1,0:T(2,128)}, f32[2,4096,128]{2,1,0:T(8,128)}) conditional(s32[]{:T(128)} %convert_element_type.69, (s32[]{:T(128)}, s32[]{:T(128)}, f32[2,4096]{1,0:T(2,128)S(1)}, bf16[2,4096,128]{2,1,0:T(8,128)(2,1)}, bf16[512,2,128]{0,2,1:T(8,128)(2,1)S(1)}, /*index=5*/f32[2,4096]{1,0:T(2,128)}, ...), branch_computations={%region_4.8_spmd, %region_9.11_spmd} | conditional | flops 2206220288 | bytes 137633952 | solution.py:168
  1116.7 2.3 multiply_reduce_fusion
  1119.0 2.8 multiply_reduce_fusion.1
  1124.7 4.4 convolution_add_fusion.1
  1130.0 1.6 slice_select_fusion
  1131.7 2.2 pad_maximum_fusion
  1139.6 20.6 %conditional.3 = (f32[2,4096]{1,0:T(2,128)}, f32[2,4096]{1,0:T(2,128)}, f32[2,4096,128]{2,1,0:T(8,128)}) conditional(s32[]{:T(128)} %convert_element_type.69, (s32[]{:T(128)}, s32[]{:T(128)}, f32[2,4096]{1,0:T(2,128)S(1)}, bf16[2,4096,128]{2,1,0:T(8,128)(2,1)}, bf16[512,2,128]{0,2,1:T(8,128)(2,1)S(1)}, /*index=5*/f32[2,4096]{1,0:T(2,128)}, ...), branch_computations={%region_4.8_spmd, %region_9.11_spmd} | conditional | flops 2206220288 | bytes 137633952 | solution.py:168
  1141.0 2.3 multiply_reduce_fusion
  1143.3 2.8 multiply_reduce_fusion.1
  1149.0 4.4 convolution_add_fusion.1
  1154.4 1.6 slice_select_fusion
  1156.0 2.2 pad_maximum_fusion
  1163.9 20.6 %conditional.3 = (f32[2,4096]{1,0:T(2,128)}, f32[2,4096]{1,0:T(2,128)}, f32[2,4096,128]{2,1,0:T(8,128)}) conditional(s32[]{:T(128)} %convert_element_type.69, (s32[]{:T(128)}, s32[]{:T(128)}, f32[2,4096]{1,0:T(2,128)S(1)}, bf16[2,4096,128]{2,1,0:T(8,128)(2,1)}, bf16[512,2,128]{0,2,1:T(8,128)(2,1)S(1)}, /*index=5*/f32[2,4096]{1,0:T(2,128)}, ...), branch_computations={%region_4.8_spmd, %region_9.11_spmd} | conditional | flops 2206220288 | bytes 137633952 | solution.py:168
  1165.3 2.3 multiply_reduce_fusion
  1167.6 2.8 multiply_reduce_fusion.1
  1173.4 4.4 convolution_add_fusion.1
  1178.7 1.6 slice_select_fusion
  1180.3 2.2 pad_maximum_fusion
  1188.2 20.6 %conditional.3 = (f32[2,4096]{1,0:T(2,128)}, f32[2,4096]{1,0:T(2,128)}, f32[2,4096,128]{2,1,0:T(8,128)}) conditional(s32[]{:T(128)} %convert_element_type.69, (s32[]{:T(128)}, s32[]{:T(128)}, f32[2,4096]{1,0:T(2,128)S(1)}, bf16[2,4096,128]{2,1,0:T(8,128)(2,1)}, bf16[512,2,128]{0,2,1:T(8,128)(2,1)S(1)}, /*index=5*/f32[2,4096]{1,0:T(2,128)}, ...), branch_computations={%region_4.8_spmd, %region_9.11_spmd} | conditional | flops 2206220288 | bytes 137633952 | solution.py:168
  1189.7 2.3 multiply_reduce_fusion
  1191.9 2.8 multiply_reduce_fusion.1
  1197.7 4.4 convolution_add_fusion.1
  1203.0 1.6 slice_select_fusion
  1204.6 2.2 pad_maximum_fusion
  1212.5 20.6 %conditional.3 = (f32[2,4096]{1,0:T(2,128)}, f32[2,4096]{1,0:T(2,128)}, f32[2,4096,128]{2,1,0:T(8,128)}) conditional(s32[]{:T(128)} %convert_element_type.69, (s32[]{:T(128)}, s32[]{:T(128)}, f32[2,4096]{1,0:T(2,128)S(1)}, bf16[2,4096,128]{2,1,0:T(8,128)(2,1)}, bf16[512,2,128]{0,2,1:T(8,128)(2,1)S(1)}, /*index=5*/f32[2,4096]{1,0:T(2,128)}, ...), branch_computations={%region_4.8_spmd, %region_9.11_spmd} | conditional | flops 2206220288 | bytes 137633952 | solution.py:168
  1214.0 2.3 multiply_reduce_fusion
  1216.3 2.8 multiply_reduce_fusion.1
  1222.0 4.4 convolution_add_fusion.1
  1228.9 2.2 pad_maximum_fusion
  1233.9 2.9 fusion.41
  1237.1 1.9 copy.44
  (177 shorter events, 71.0 us)
Async XLA Ops:
  24.8 8.8 copy-start.9
  24.8 8.8 copy-start.10
  24.8 8.8 copy-start.8
  24.8 911.8 %all-to-all-start = ((bf16[8,1024,2560]{2,1,0:T(8,128)(2,1)}), bf16[8,1024,2560]{2,1,0:T(8,128)(2,1)}, u32[]{:S(2)}, u32[]{:S(2)}) async-start(bf16[8,1024,2560]{2,1,0:T(8,128)(2,1)} %stack.2), calls=%async_computation | async-start | bytes 83886080 | tf_op jit(solution)/shard_map/all_to_all | solution.py:11
  32.8 93.0 %all-gather.4.cloned.1.call-start = ((), (), s32[]{:S(2)}) async-start(), calls=%async_computation.1 | async-start | bytes 10485760 | tf_op jit(solution)/shard_map/all_gather | solution.py:90
  33.5 964.8 %all-gather.6.cloned.1.call-start = ((), (), s32[]{:S(2)}) async-start(), calls=%async_computation.2 | async-start | bytes 2359296 | tf_op jit(solution)/shard_map/all_gather | solution.py:145
  936.6 33.6 %copy-start.7 = (bf16[2048]{0:T(1024)(128)(2,1)S(1)}, bf16[2048]{0:T(1024)(128)(2,1)}, u32[]{:S(2)}) copy-start(bf16[2048]{0:T(1024)(128)(2,1)} %param.17) | copy-start | bytes 12292
  969.5 59.0 %all-gather.8.cloned.1.call-start = ((), (), s32[]{:S(2)}) async-start(), calls=%async_computation.3 | async-start | bytes 2359296 | tf_op jit(solution)/shard_map/all_gather | solution.py:146
  1034.3 1.7 copy-start.5
  1041.9 7.2 copy-start.3
  1043.8 5.3 copy-start.6
  1070.4 4.3 copy-start
  1073.1 2.0 copy-start.2
  1076.1 4.4 copy-start.1
  1076.1 5.3 copy-start.4
  1094.7 4.3 copy-start
  1097.5 2.0 copy-start.2
  1100.4 4.4 copy-start.1
  1100.4 5.3 copy-start.4
  1119.0 4.3 copy-start
  1121.8 2.0 copy-start.2
  1124.7 4.4 copy-start.1
  1124.7 5.3 copy-start.4
  1143.3 4.3 copy-start
  1146.1 2.0 copy-start.2
  1149.0 4.4 copy-start.1
  1149.0 5.3 copy-start.4
  1167.6 4.3 copy-start
  1170.4 2.0 copy-start.2
  1173.3 4.4 copy-start.1
  1173.3 5.3 copy-start.4
  1191.9 4.3 copy-start
  1194.7 2.0 copy-start.2
  1197.6 4.4 copy-start.1
  1197.7 5.3 copy-start.4
  1216.2 4.3 copy-start
  1219.0 2.0 copy-start.2
  1222.0 4.4 copy-start.1
  1222.0 5.3 copy-start.4
Sparse Core Ops, SparseCore 0:
  35.5 90.3 all-gather.3
  969.7 28.6 all-gather.5
  999.9 28.5 all-gather.7
